TPU v7x, 32 devices: a whole 2x2x4 slice. The times are simulated.
32 devices in a mesh: tok: 8 (over z, x), exp: 4 (over y, core).
Axes of the slice: x: 2, y: 2, z: 4, core: 2. Of those that a mesh axis runs over, the one named last changes fastest.
Arguments:
- tokens: bfloat16 [16384, 7168], P('tok', 'exp'), may hold values from -6 to 6
- gate_weight: bfloat16 [7168, 256], P('exp'), may hold values from -0.0625 to 0.0625
- expert_ids: int32 [16384, 8], P('tok'), may hold values from 0 to 255, all different within a row
- expert_bias: float32 [256], P('exp'), may hold values from -0.002 to 0.002
Outputs:
- affinities: float32 [16384, 256], P('tok', 'exp')
- weights: float32 [16384, 8], P('tok')
- load: float32 [256], replicated
- new_bias: float32 [256], replicated
All inputs are finite; a program needn't handle non-finite values.
Results may differ from a plain program's by a relative error of at most 0.0003.
Values may be sent and summed in bfloat16 or wider, within the bound.
A program may use at most 64 MiB of HBM per device.

v0:
```python
import functools

import jax
import jax.numpy as jnp
from jax import lax
from jax.experimental import pallas as pl
from jax.experimental.pallas import tpu as pltpu
from jax.sharding import PartitionSpec as P

MESH = pl.DeviceIdType.MESH
F32 = jnp.float32
LINK = jnp.int16
TOP_CODE = 32760.0
TOKEN_BOUND, GATE_BOUND = 6.0, 0.0625


def kernel(ntok, widths, x_hbm, w_hbm, ids_hbm, bias_hbm,
           affv, wtsv, load_ref, newb_ref,
           xv, wv, wt, ids, bias_own, bias_all, part, rx1, keep, tx2, rx2, mine, lin, lrx,
           cnt_a, cnt,
           x_sem, w_sem, i_sem, b_sem, s1, r1, s2, r2, s4, r4, sa, ra, sc, rc, sb, rb):
    own = bias_own.shape[1]
    n = len(widths)
    starts = [sum(widths[:i]) for i in range(n)]
    t, e = lax.axis_index("tok"), lax.axis_index("exp")
    y, c = e // 2, e % 2
    mate = 2 * y + 1 - c
    peer = 2 * (1 - y) + c
    cross = 2 * (1 - y) + 1 - c
    experts = 4 * own

    def cols(i):
        return pl.ds(starts[i], widths[i])

    ids_in = pltpu.make_async_copy(ids_hbm, ids, i_sem)
    b_in = pltpu.make_async_copy(bias_hbm, bias_own, b_sem)
    w_in = pltpu.make_async_copy(w_hbm, wv, w_sem)
    x_in = [pltpu.make_async_copy(x_hbm.at[cols(i)], xv.at[cols(i)], x_sem.at[i]) for i in range(n)]
    w_in.start()
    ids_in.start()
    b_in.start()
    ahead = 2
    for copy in x_in[:ahead]:
        copy.start()

    barrier = pltpu.get_barrier_semaphore()
    for other in (mate, peer, cross):
        pl.semaphore_signal(barrier, inc=1, device_id=(t, other), device_id_type=MESH)
    for d in range(1, ntok):
        pl.semaphore_signal(barrier, inc=1, device_id=((t + d) % ntok, e), device_id_type=MESH)

    ids_in.wait()
    lanes = 128
    share = ids.shape[1] // 4
    numbers = lax.broadcasted_iota(jnp.int32, (experts, lanes), 0).astype(F32).astype(jnp.bfloat16)
    one, zero = jnp.bfloat16(1), jnp.bfloat16(0)
    acc = jnp.zeros((experts, lanes), jnp.bfloat16)
    for g in range(share // lanes):
        at = pl.multiple_of(e * share + g * lanes, lanes)
        found = ids[:, pl.ds(at, lanes)].astype(F32).astype(jnp.bfloat16)
        for j in range(ids.shape[0]):
            acc = acc + jnp.where(found[j:j + 1] == numbers, one, zero)
    counts = lax.dot_general(jnp.ones((8, lanes), jnp.bfloat16), acc,
                             (((1,), (1,)), ((), ())), preferred_element_type=F32)
    cnt_a[0] = counts.astype(jnp.int32)
    b_in.wait()
    bias_all[0] = jnp.broadcast_to(bias_own[...], bias_all.shape[1:])
    w_in.wait()
    for copy in x_in[ahead:2 * ahead]:
        copy.start()
    wt[...] = wv[...].T

    pl.semaphore_wait(barrier, 3 + ntok - 1)

    group = ((1, mate), (2, peer), (3, cross))
    share_out = [pltpu.make_async_remote_copy(
        src_ref=cnt_a.at[0], dst_ref=cnt_a.at[k], send_sem=sa.at[k], recv_sem=ra.at[k],
        device_id=(t, other), device_id_type=MESH) for k, other in group]
    bias_out = [pltpu.make_async_remote_copy(
        src_ref=bias_own, dst_ref=bias_all.at[k, pl.ds(0, 1)], send_sem=sb.at[k], recv_sem=rb.at[k],
        device_id=(t, other), device_id_type=MESH) for k, other in group]
    cnt_out = [pltpu.make_async_remote_copy(
        src_ref=cnt.at[0], dst_ref=cnt.at[d], send_sem=sc.at[d], recv_sem=rc.at[d],
        device_id=((t + d) % ntok, e), device_id_type=MESH) for d in range(1, ntok)]
    for copy in share_out + bias_out:
        copy.start()

    def first(i):
        return pltpu.make_async_remote_copy(
            src_ref=part.at[:, 1 - c, :, cols(i)], dst_ref=rx1.at[:, :, cols(i)],
            send_sem=s1.at[i], recv_sem=r1.at[i], device_id=(t, mate), device_id_type=MESH)

    def second(i):
        return pltpu.make_async_remote_copy(
            src_ref=tx2.at[:, cols(i)], dst_ref=rx2.at[:, cols(i)],
            send_sem=s2.at[i], recv_sem=r2.at[i], device_id=(t, peer), device_id_type=MESH)

    def fourth(i):
        return pltpu.make_async_remote_copy(
            src_ref=lin.at[:, cols(i)], dst_ref=lrx.at[:, cols(i)],
            send_sem=s4.at[i], recv_sem=r4.at[i], device_id=(t, mate), device_id_type=MESH)

    local = lax.broadcasted_iota(jnp.int32, (own, 1), 0)

    def pick(i, values, block):
        rows = []
        base = local + block * own
        for j in range(ids.shape[0]):
            hit = ids[j:j + 1, cols(i)] == base
            rows.append(jnp.sum(jnp.where(hit, values, F32(0)), axis=0, keepdims=True))
        return jnp.concatenate(rows, axis=0)

    def stage_a(i):
        x_in[i].wait()
        if i + 2 * ahead < n:
            x_in[i + 2 * ahead].start()
        r = lax.dot_general(wt[...], xv[cols(i)], (((1,), (1,)), ((), ())), preferred_element_type=F32)
        part[:, :, :, cols(i)] = r.reshape(2, 2, own, widths[i])
        first(i).start()

    grain = float(int(30000 / (2 * xv.shape[1] * TOKEN_BOUND * GATE_BOUND)))

    def step_of(whole):
        return whole * F32(1.0 / (grain * TOP_CODE))

    def stage_b(i):
        first(i).wait_recv()
        give = part[1 - y, c, :, cols(i)] + rx1[1 - y, :, cols(i)]
        held = part[y, c, :, cols(i)] + rx1[y, :, cols(i)]
        keep[:, cols(i)] = held
        largest = jnp.max(jnp.maximum(jnp.abs(give), jnp.abs(held)), axis=0, keepdims=True)
        whole = jnp.floor(largest * grain) + 1.0
        inverse = F32(grain * TOP_CODE) / whole
        code = jnp.round(give * inverse)
        chosen = jnp.round(pick(i, held, e) * inverse)
        tail = jnp.concatenate([chosen, jnp.broadcast_to(whole, chosen.shape)], axis=0)
        tx2[0:own, cols(i)] = code.astype(jnp.int32).astype(LINK)
        tx2[own:, cols(i)] = tail.astype(jnp.int32).astype(LINK)
        second(i).start()
        lin[:, cols(i)] = pick(i, code, peer) * step_of(whole)
        mine[:, cols(i)] = chosen * step_of(whole)

    def stage_c(i):
        second(i).wait_recv()
        code = rx2[0:own, cols(i)].astype(jnp.int32).astype(F32)
        tail = rx2[own:, cols(i)].astype(jnp.int32).astype(F32)
        top = ids.shape[0]
        step = step_of(tail[top:top + 1])
        logits = keep[:, cols(i)] + code * step
        ours = mine[:, cols(i)] + pick(i, code, e) * step
        theirs = lin[:, cols(i)] + tail[0:top] * step
        lin[:, cols(i)] = ours + theirs
        fourth(i).start()
        affv[:, cols(i)] = 1.0 / (1.0 + jnp.exp(-logits))

    def stage_d(i):
        fourth(i).wait_recv()
        chosen = 1.0 / (1.0 + jnp.exp(-(lin[:, cols(i)] + lrx[:, cols(i)])))
        wtsv[:, cols(i)] = 2.5 * chosen / jnp.sum(chosen, axis=0, keepdims=True)

    def merge_counts():
        for copy in share_out:
            copy.wait()
        cnt[0] = (cnt_a[0] + cnt_a[1]) + (cnt_a[2] + cnt_a[3])
        for copy in cnt_out:
            copy.start()

    def finish_counts():
        for copy in cnt_out + bias_out:
            copy.wait()
        total = cnt[0]
        for d in range(1, ntok):
            total = total + cnt[d]
        load = total[0:1].astype(F32)
        load_ref[...] = load
        target = F32(ntok * ids.shape[1] * ids.shape[0])
        gap = target - F32(experts) * load
        sign = jnp.where(gap > 0, F32(1), jnp.where(gap < 0, F32(-1), F32(0)))
        b0, b1, b2, b3 = (bias_all[k, 0:1] for k in range(4))
        near = jnp.where(c == 0, b0, b1), jnp.where(c == 0, b1, b0)
        far = jnp.where(c == 0, b2, b3), jnp.where(c == 0, b3, b2)
        low = [jnp.where(y == 0, p, q) for p, q in zip(near, far)]
        high = [jnp.where(y == 0, q, p) for p, q in zip(near, far)]
        bias = jnp.concatenate(low + high, axis=1)
        newb_ref[...] = bias + 0.001 * sign

    lag_b, lag_c, lag_d = 2, 7, 8
    for step in range(n + lag_d):
        if step < n:
            stage_a(step)
        if 0 <= step - lag_b < n:
            stage_b(step - lag_b)
        if step == n // 2:
            merge_counts()
        if step == n + lag_b:
            finish_counts()
        if 0 <= step - lag_c < n:
            stage_c(step - lag_c)
        if 0 <= step - lag_d < n:
            stage_d(step - lag_d)
    for i in range(n):
        first(i).wait_send()
        second(i).wait_send()
        fourth(i).wait_send()


def place(aff, wts, load, newb, aff_hbm, wts_hbm, load_hbm, newb_hbm, sem):
    copies = [pltpu.make_async_copy(a, b, sem.at[k]) for k, (a, b) in enumerate(
        ((aff, aff_hbm), (wts, wts_hbm), (load, load_hbm), (newb, newb_hbm)))]
    for copy in copies:
        copy.start()
    for copy in copies:
        copy.wait()


def local(ntok, tokens, gate_weight, expert_ids, expert_bias):
    rows, depth = tokens.shape
    experts = gate_weight.shape[1]
    own = expert_bias.shape[0]
    top = expert_ids.shape[1]
    piece = 256
    widths = [piece // 2] * 2 + [piece] * (rows // piece - 1)
    n = len(widths)
    dma = pltpu.SemaphoreType.DMA
    vm = pltpu.VMEM
    any_ = pl.BlockSpec(memory_space=pl.ANY)
    vmem = pl.BlockSpec(memory_space=pltpu.VMEM)
    shapes = ((own, rows), (top, rows), (1, experts), (1, experts))
    results = pl.pallas_call(
        functools.partial(kernel, ntok, widths),
        out_shape=tuple(pltpu.VMEM(shape, F32) for shape in shapes),
        in_specs=[any_] * 4,
        out_specs=(vmem,) * 4,
        scratch_shapes=[
            vm((rows, depth), tokens.dtype), vm((depth, experts), gate_weight.dtype),
            vm((experts, depth), gate_weight.dtype), vm((top, rows), jnp.int32),
            vm((1, own), F32), vm((4, 8, own), F32),
            vm((2, 2, own, rows), F32), vm((2, own, rows), F32), vm((own, rows), F32),
            vm((own + 2 * top, rows), LINK), vm((own + 2 * top, rows), LINK),
            vm((top, rows), F32), vm((top, rows), F32), vm((top, rows), F32),
            vm((4, 8, experts), jnp.int32), vm((ntok, 8, experts), jnp.int32),
            dma((n,)), dma, dma, dma, dma((n,)), dma((n,)), dma((n,)), dma((n,)),
            dma((n,)), dma((n,)), dma((4,)), dma((4,)), dma((ntok,)), dma((ntok,)), dma((4,)), dma((4,)),
        ],
        compiler_params=pltpu.CompilerParams(
            collective_id=0, has_side_effects=True, vmem_limit_bytes=60 * 1024 * 1024),
    )(tokens, gate_weight, expert_ids.T, expert_bias.reshape(1, own))
    aff, wts, load, newb = pl.pallas_call(
        place,
        out_shape=tuple(jax.ShapeDtypeStruct(shape, F32) for shape in shapes),
        in_specs=[vmem] * 4,
        out_specs=(pl.BlockSpec(memory_space=pltpu.HBM),) * 4,
        scratch_shapes=[dma((4,))],
    )(*(pltpu.with_memory_space_constraint(r, pltpu.VMEM) for r in results))
    return aff.T, wts.T, load.reshape(experts), newb.reshape(experts)


def solution(mesh):
    in_specs = (P("tok", "exp"), P("exp", None), P("tok", None), P("exp"))
    out_specs = (P("tok", "exp"), P("tok", None), P(), P())
    return jax.shard_map(functools.partial(local, mesh.shape["tok"]), mesh=mesh,
                         in_specs=in_specs, out_specs=out_specs, check_vma=False)
```

profile of v0, /device:TPU:1, one launch (start us, length us, event | category | flops | bytes accessed | tf_op | source)
XLA Modules:
  0.0 21.4 jit_solution(15237611040800737802)
XLA Ops:
  0.6 19.9 %shard_map.75 = (f32[64,2048]{1,0:T(8,128)S(1)}, f32[8,2048]{1,0:T(8,128)S(1)}, f32[1,256]{1,0:T(1,128)S(1)}, f32[1,256]{1,0:T(1,128)S(1)}) custom-call(bf16[2048,1792]{1,0:T(8,128)(2,1)} %x_hbm.1, bf16[1792,256]{1,0:T(8,128)(2,1)} %w_hbm.1, s32[8,2048]{1,0:T(8,128)} %bitcast.6, f32[1,64]{1,0:T(1,128)} %bitcast.7), custom_call_target="tpu_custom_call" | custom-call | tf_op jit(solution)/shard_map/pallas_call | solution.py:229
  20.5 0.8 %shard_map.76 = (f32[64,2048]{1,0:T(8,128)}, f32[8,2048]{1,0:T(8,128)}, f32[1,256]{1,0:T(1,128)}, f32[1,256]{1,0:T(1,128)}) custom-call(f32[64,2048]{1,0:T(8,128)S(1)} %get-tuple-element.12.aff, f32[8,2048]{1,0:T(8,128)S(1)} %get-tuple-element.13.wts, f32[1,256]{1,0:T(1,128)S(1)} %get-tuple-element.14.load, f32[1,256]{1,0:T(1,128)S(1)} %get-tuple-element.15.newb), custom_call_target="tpu_custom_call" | custom-call | tf_op jit(solution)/shard_map/pallas_call | solution.py:248
where the time goes:
time: 21.6 us; the launch traced here: 21.4 us
  Pallas kernels  20.7 us (96%)
  between operations  0.64 us (3%)
    pallas_call x1, Pallas kernels, local(): pl.pallas_call(functools.partial(kernel, ntok, widths), out_shape=tuple((...  19.9 us
    pallas_call x1, Pallas kernels, local(): pl.pallas_call(place, out_shape=tuple((jax.ShapeDtypeStruct(shape, F32) f...  0.84 us

commit v1 on v0

v1 whole, which is shorter than its diff:
```python
import functools

import jax
import jax.numpy as jnp
from jax import lax
from jax.experimental import pallas as pl
from jax.experimental.pallas import tpu as pltpu
from jax.sharding import PartitionSpec as P

MESH = pl.DeviceIdType.MESH
F32 = jnp.float32
LINK = jnp.int16
TOP_CODE = 32760.0
TOKEN_BOUND, GATE_BOUND = 6.0, 0.0625
ROOT = 1


def kernel(ntok, widths, x_hbm, w_hbm, ids_hbm, bias_hbm,
           affv, wtsv, load_ref, newb_ref,
           xv, wv, wt, ids, bias_own, bias_all, part, rx1, keep, mine, tx2, rx2, cnt, fin,
           x_sem, w_sem, i_sem, b_sem, s1, r1, s2, r2, sc, rc, sb, rb, sf, rf, ready):
    own = bias_own.shape[1]
    top, rows = ids.shape
    n = len(widths)
    starts = [sum(widths[:i]) for i in range(n)]
    t, e = lax.axis_index("tok"), lax.axis_index("exp")
    y, c = e // 2, e % 2
    mate = 2 * y + 1 - c
    peer = 2 * (1 - y) + c
    experts = 4 * own
    is_root = e == ROOT
    others = [k for k in range(4) if k != ROOT]

    def cols(i):
        return pl.ds(starts[i], widths[i])

    ids_in = pltpu.make_async_copy(ids_hbm, ids, i_sem)
    b_in = pltpu.make_async_copy(bias_hbm, bias_own, b_sem)
    w_in = pltpu.make_async_copy(w_hbm, wv, w_sem)
    x_in = [pltpu.make_async_copy(x_hbm.at[cols(i)], xv.at[cols(i)], x_sem.at[i]) for i in range(n)]
    ids_in.start()
    w_in.start()
    b_in.start()
    ahead = 2
    for copy in x_in[:ahead]:
        copy.start()

    barrier = pltpu.get_barrier_semaphore()

    for k in others:
        @pl.when(e != k)
        def _():
            pl.semaphore_signal(barrier, inc=1, device_id=(t, k), device_id_type=MESH)

    @pl.when(is_root)
    def _():
        for d in range(1, ntok):
            pl.semaphore_signal(barrier, inc=1, device_id=((t + d) % ntok, e), device_id_type=MESH)

    ids_in.wait()
    b_in.wait()

    @pl.when(is_root)
    def _():
        lanes = 128
        numbers = lax.broadcasted_iota(jnp.int32, (experts, lanes), 0).astype(F32).astype(jnp.bfloat16)
        one, zero = jnp.bfloat16(1), jnp.bfloat16(0)
        chunk = 256 // top
        groups = rows // lanes
        total = jnp.zeros((8, experts), F32)
        for g0 in range(0, groups, chunk):
            acc = jnp.zeros((experts, lanes), jnp.bfloat16)
            for g in range(g0, min(g0 + chunk, groups)):
                found = ids[:, pl.ds(g * lanes, lanes)].astype(F32).astype(jnp.bfloat16)
                for j in range(top):
                    acc = acc + jnp.where(found[j:j + 1] == numbers, one, zero)
            total = total + lax.dot_general(jnp.ones((8, lanes), jnp.bfloat16), acc,
                                            (((1,), (1,)), ((), ())), preferred_element_type=F32)
        cnt[0] = total[0:1].astype(jnp.int32)
        bias_all[ROOT] = bias_own[...]

    w_in.wait()
    for copy in x_in[ahead:2 * ahead]:
        copy.start()
    wt[...] = wv[...].T

    bias_out = pltpu.make_async_remote_copy(
        src_ref=bias_own, dst_ref=bias_all.at[e], send_sem=sb, recv_sem=rb.at[e],
        device_id=(t, ROOT), device_id_type=MESH)
    bias_back = [pltpu.make_async_remote_copy(
        src_ref=bias_own, dst_ref=bias_all.at[k], send_sem=sb, recv_sem=rb.at[k],
        device_id=(t, k), device_id_type=MESH) for k in others]
    cnt_out = [pltpu.make_async_remote_copy(
        src_ref=cnt.at[0], dst_ref=cnt.at[d], send_sem=sc.at[d], recv_sem=rc.at[d],
        device_id=((t + d) % ntok, e), device_id_type=MESH) for d in range(1, ntok)]
    fin_out = [pltpu.make_async_remote_copy(
        src_ref=fin, dst_ref=fin, send_sem=sf.at[k], recv_sem=rf,
        device_id=(t, k), device_id_type=MESH) for k in others]

    @pl.when(jnp.logical_not(is_root))
    def _():
        pl.semaphore_wait(barrier, 3)
        pl.semaphore_signal(ready.at[e], inc=1, device_id=(t, ROOT), device_id_type=MESH)
        bias_out.start()

    @pl.when(is_root)
    def _():
        for k in others:
            pl.semaphore_wait(ready.at[k], 1)

    def send_counts():
        pl.semaphore_wait(barrier, ntok - 1)
        for copy in cnt_out:
            copy.start()

    def send_counts_soon():
        pl.when(jnp.logical_and(is_root, 2 * t >= ntok))(send_counts)

    def send_counts_late():
        pl.when(jnp.logical_and(is_root, 2 * t < ntok))(send_counts)

    def finish_counts():
        @pl.when(is_root)
        def _():
            for copy in cnt_out + bias_back:
                copy.wait_recv()
            total = cnt[0]
            for d in range(1, ntok):
                total = total + cnt[d]
            load = total.astype(F32)
            target = F32(ntok * rows * top)
            gap = target - F32(experts) * load
            sign = jnp.where(gap > 0, F32(1), jnp.where(gap < 0, F32(-1), F32(0)))
            bias = jnp.concatenate([bias_all[k] for k in range(4)], axis=1)
            fin[0] = load
            fin[1] = bias + 0.001 * sign
            for copy in fin_out:
                copy.start()

    def close_counts():
        @pl.when(is_root)
        def _():
            for copy in cnt_out + fin_out:
                copy.wait_send()

        @pl.when(jnp.logical_not(is_root))
        def _():
            fin_out[0].wait_recv()
            bias_out.wait_send()

        load_ref[...] = fin[0]
        newb_ref[...] = fin[1]

    def first(i):
        return pltpu.make_async_remote_copy(
            src_ref=part.at[1 - c, :, cols(i)], dst_ref=rx1.at[:, cols(i)],
            send_sem=s1.at[i], recv_sem=r1.at[i], device_id=(t, mate), device_id_type=MESH)

    def second(i):
        return pltpu.make_async_remote_copy(
            src_ref=tx2.at[:, cols(i)], dst_ref=rx2.at[:, cols(i)],
            send_sem=s2.at[i], recv_sem=r2.at[i], device_id=(t, peer), device_id_type=MESH)

    def stage_a(i):
        x_in[i].wait()
        if i + 2 * ahead < n:
            x_in[i + 2 * ahead].start()
        r = lax.dot_general(wt[...], xv[cols(i)], (((1,), (1,)), ((), ())), preferred_element_type=F32)
        for k in range(4):
            part[k % 2, pl.ds(k // 2 * own, own), cols(i)] = r[k * own:(k + 1) * own]
        mine_ids = ids[:, cols(i)]
        low, high = mine_ids & 7, mine_ids >> 3
        picked = jnp.zeros(mine_ids.shape, F32)
        for g in range(experts // 8):
            at = jnp.take_along_axis(r[8 * g:8 * g + 8], low, axis=0, mode="promise_in_bounds")
            picked = jnp.where(high == g, at, picked)
        for k in range(2):
            part[k, pl.ds(2 * own, top), cols(i)] = picked
        first(i).start()

    bound = 2 * xv.shape[1] * TOKEN_BOUND * GATE_BOUND
    grain = TOP_CODE / bound ** 0.25

    def encode(v):
        size = lax.rsqrt(lax.rsqrt(jnp.abs(v) + F32(1e-30))) * F32(grain) + F32(0.5)
        return jnp.where(v < 0, -size, size).astype(jnp.int32)

    def decode(whole):
        u = whole.astype(F32)
        return (u * u * F32(grain ** -4)) * (u * jnp.abs(u))

    def stage_b(i):
        first(i).wait_recv()
        theirs = pl.ds(pl.multiple_of((1 - y) * own, own), own)
        ours = pl.ds(pl.multiple_of(y * own, own), own)
        tops = pl.ds(2 * own, top)
        code = encode(part[c, theirs, cols(i)] + rx1[theirs, cols(i)])
        chosen = encode(part[c, tops, cols(i)] + rx1[tops, cols(i)])
        tx2[0:own, cols(i)] = code.astype(LINK)
        tx2[own:, cols(i)] = chosen.astype(LINK)
        second(i).start()
        keep[:, cols(i)] = part[c, ours, cols(i)] + rx1[ours, cols(i)]
        mine[:, cols(i)] = decode(chosen)

    def stage_c(i):
        second(i).wait_recv()
        code = decode(rx2[0:own, cols(i)].astype(jnp.int32))
        tail = decode(rx2[own:, cols(i)].astype(jnp.int32))
        chosen = 1.0 / (1.0 + jnp.exp(-(mine[:, cols(i)] + tail)))
        wtsv[:, cols(i)] = 2.5 * chosen / jnp.sum(chosen, axis=0, keepdims=True)
        affv[:, cols(i)] = 1.0 / (1.0 + jnp.exp(-(keep[:, cols(i)] + code)))

    lag_b = 3
    for step in range(n + lag_b):
        if step < n:
            stage_a(step)
        if step == lag_b - 1:
            send_counts_soon()
        if 0 <= step - lag_b < n:
            stage_b(step - lag_b)
    send_counts_late()
    for i in range(n):
        if i == n - 2:
            finish_counts()
        stage_c(i)
    close_counts()
    for i in range(n):
        first(i).wait_send()
        second(i).wait_send()


def place(aff, wts, load, newb, aff_hbm, wts_hbm, load_hbm, newb_hbm, sem):
    copies = [pltpu.make_async_copy(a, b, sem.at[k]) for k, (a, b) in enumerate(
        ((aff, aff_hbm), (wts, wts_hbm), (load, load_hbm), (newb, newb_hbm)))]
    for copy in copies:
        copy.start()
    for copy in copies:
        copy.wait()


def local(ntok, tokens, gate_weight, expert_ids, expert_bias):
    rows, depth = tokens.shape
    experts = gate_weight.shape[1]
    own = expert_bias.shape[0]
    top = expert_ids.shape[1]
    piece = 256
    widths = [piece // 2] * 2 + [piece] * (rows // piece - 1)
    n = len(widths)
    dma = pltpu.SemaphoreType.DMA
    vm = pltpu.VMEM
    any_ = pl.BlockSpec(memory_space=pl.ANY)
    vmem = pl.BlockSpec(memory_space=pltpu.VMEM)
    shapes = ((own, rows), (top, rows), (1, experts), (1, experts))
    results = pl.pallas_call(
        functools.partial(kernel, ntok, widths),
        out_shape=tuple(pltpu.VMEM(shape, F32) for shape in shapes),
        in_specs=[any_] * 4,
        out_specs=(vmem,) * 4,
        scratch_shapes=[
            vm((rows, depth), tokens.dtype), vm((depth, experts), gate_weight.dtype),
            vm((experts, depth), gate_weight.dtype), vm((top, rows), jnp.int32),
            vm((1, own), F32), vm((4, 1, own), F32),
            vm((2, 2 * own + top, rows), F32), vm((2 * own + top, rows), F32),
            vm((own, rows), F32), vm((top, rows), F32),
            vm((own + top, rows), LINK), vm((own + top, rows), LINK),
            vm((ntok, 1, experts), jnp.int32), vm((2, 1, experts), F32),
            dma((n,)), dma, dma, dma, dma((n,)), dma((n,)), dma((n,)), dma((n,)),
            dma((ntok,)), dma((ntok,)), dma, dma((4,)), dma((4,)), dma,
            pltpu.SemaphoreType.REGULAR((4,)),
        ],
        compiler_params=pltpu.CompilerParams(
            collective_id=0, has_side_effects=True, vmem_limit_bytes=60 * 1024 * 1024),
    )(tokens, gate_weight, expert_ids.T, expert_bias.reshape(1, own))
    aff, wts, load, newb = pl.pallas_call(
        place,
        out_shape=tuple(jax.ShapeDtypeStruct(shape, F32) for shape in shapes),
        in_specs=[vmem] * 4,
        out_specs=(pl.BlockSpec(memory_space=pltpu.HBM),) * 4,
        scratch_shapes=[dma((4,))],
    )(*(pltpu.with_memory_space_constraint(r, pltpu.VMEM) for r in results))
    return aff.T, wts.T, load.reshape(experts), newb.reshape(experts)


def solution(mesh):
    in_specs = (P("tok", "exp"), P("exp", None), P("tok", None), P("exp"))
    out_specs = (P("tok", "exp"), P("tok", None), P(), P())
    return jax.shard_map(functools.partial(local, mesh.shape["tok"]), mesh=mesh,
                         in_specs=in_specs, out_specs=out_specs, check_vma=False)
```

time: 21.6 us -> 17.4 us (0.81)
  the two profiles are of different devices: /device:TPU:1 before, /device:TPU:0 now
where the time goes in v1:
time: 17.4 us; the launch traced here: 17.3 us
  Pallas kernels  16.6 us (95%)
  between operations  0.64 us (4%)
    pallas_call x1, Pallas kernels, local(): pl.pallas_call(functools.partial(kernel, ntok, widths), out_shape=tuple((...  15.8 us
    pallas_call x1, Pallas kernels, local(): pl.pallas_call(place, out_shape=tuple((jax.ShapeDtypeStruct(shape, F32) f...  0.84 us

profile of v1, /device:TPU:0, one launch (start us, length us, event | category | flops | bytes accessed | tf_op | source)
XLA Modules:
  0.0 17.3 jit_solution(10893835116682602005)
XLA Ops:
  0.6 15.8 %shard_map.75 = (f32[64,2048]{1,0:T(8,128)S(1)}, f32[8,2048]{1,0:T(8,128)S(1)}, f32[1,256]{1,0:T(1,128)S(1)}, f32[1,256]{1,0:T(1,128)S(1)}) custom-call(bf16[2048,1792]{1,0:T(8,128)(2,1)} %x_hbm.1, bf16[1792,256]{1,0:T(8,128)(2,1)} %w_hbm.1, s32[8,2048]{1,0:T(8,128)} %bitcast.6, f32[1,64]{1,0:T(1,128)} %bitcast.7), custom_call_target="tpu_custom_call" | custom-call | tf_op jit(solution)/shard_map/pallas_call | solution.py:254
  16.4 0.8 %shard_map.76 = (f32[64,2048]{1,0:T(8,128)}, f32[8,2048]{1,0:T(8,128)}, f32[1,256]{1,0:T(1,128)}, f32[1,256]{1,0:T(1,128)}) custom-call(f32[64,2048]{1,0:T(8,128)S(1)} %get-tuple-element.12.aff, f32[8,2048]{1,0:T(8,128)S(1)} %get-tuple-element.13.wts, f32[1,256]{1,0:T(1,128)S(1)} %get-tuple-element.14.load, f32[1,256]{1,0:T(1,128)S(1)} %get-tuple-element.15.newb), custom_call_target="tpu_custom_call" | custom-call | tf_op jit(solution)/shard_map/pallas_call | solution.py:274

commit v2 on v1

v2 whole, which is shorter than its diff:
```python
import functools

import jax
import jax.numpy as jnp
from jax import lax
from jax.experimental import pallas as pl
from jax.experimental.pallas import tpu as pltpu
from jax.sharding import PartitionSpec as P

MESH = pl.DeviceIdType.MESH
F32 = jnp.float32
LINK = jnp.int16
TOP_CODE = 32760.0
TOKEN_BOUND, GATE_BOUND = 6.0, 0.0625
W_CHUNKS = 4
ROOT = 1


def plan(n, ahead):
    order = [("a", i) for i in range(ahead)]
    for i in range(n):
        order += [("b", i)] + ([("a", i + ahead)] if i + ahead < n else [])
    return order


def kernel(ntok, widths, x_hbm, w_hbm, ids_hbm, bias_hbm,
           affv, wtsv, load_ref, newb_ref,
           xv, wv, ids, bias_all, part, rx1, keep, mine, tx2, rx2, cnt, fin,
           l_sem, s1, r1, s2, r2, sc, rc, rb, ready):
    sizes = sorted(set(widths))
    acc_of = []
    for i, width in enumerate(widths):
        acc_of.append(2 * sizes.index(width) + sum(w == width for w in widths[:i]) % 2)
    specs = [tuple(pltpu.ACC(q)((width, 256), F32) for q in (0, 1)) for width in sizes for _ in range(2)]
    pl.run_scoped(functools.partial(body, ntok, widths, acc_of, (
        x_hbm, w_hbm, ids_hbm, bias_hbm, affv, wtsv, load_ref, newb_ref,
        xv, wv, ids, bias_all, part, rx1, keep, mine, tx2, rx2, cnt, fin,
        l_sem, s1, r1, s2, r2, sc, rc, rb, ready)), *specs)


def body(ntok, widths, acc_of, refs, *accs):
    (x_hbm, w_hbm, ids_hbm, bias_hbm, affv, wtsv, load_ref, newb_ref,
     xv, wv, ids, bias_all, part, rx1, keep, mine, tx2, rx2, cnt, fin,
     l_sem, s1, r1, s2, r2, sc, rc, rb, ready) = refs
    own = bias_all.shape[2]
    top, rows = ids.shape
    depth = xv.shape[1]
    n = len(widths)
    starts = [sum(widths[:i]) for i in range(n)]
    t, e = lax.axis_index("tok"), lax.axis_index("exp")
    y, c = e // 2, e % 2
    mate = 2 * y + 1 - c
    peer = 2 * (1 - y) + c
    experts = 4 * own
    is_root = e == ROOT
    others = [k for k in range(4) if k != ROOT]

    def cols(i):
        return pl.ds(starts[i], widths[i])

    chunk = -(-depth // W_CHUNKS // 256) * 256
    chunks = [pl.ds(k, min(chunk, depth - k)) for k in range(0, depth, chunk)]
    nw = len(chunks)
    w_in = [pltpu.make_async_copy(w_hbm.at[k], wv.at[k], l_sem.at[j]) for j, k in enumerate(chunks)]
    first_x = 3
    slot = [nw + i if i < first_x else (i - first_x) % (nw + first_x) for i in range(n)]
    x_in = [pltpu.make_async_copy(x_hbm.at[cols(i)], xv.at[cols(i)], l_sem.at[slot[i]]) for i in range(n)]
    ids_in = pltpu.make_async_copy(ids_hbm, ids, l_sem.at[nw + first_x])
    ids_in.start()
    for copy in w_in + x_in[:first_x]:
        copy.start()

    barrier = pltpu.get_barrier_semaphore()

    for k in others:
        @pl.when(e != k)
        def _():
            pl.semaphore_signal(barrier, inc=1, device_id=(t, k), device_id_type=MESH)

    bias_in = pltpu.make_async_copy(bias_hbm, bias_all.at[ROOT], sc)
    bias_out = pltpu.make_async_remote_copy(
        src_ref=bias_hbm, dst_ref=bias_all.at[e], send_sem=sc, recv_sem=rb,
        device_id=(t, ROOT), device_id_type=MESH)
    bias_back = pltpu.make_async_remote_copy(
        src_ref=bias_all.at[pl.ds(0, 3)], dst_ref=bias_all.at[pl.ds(0, 3)], send_sem=sc, recv_sem=rb,
        device_id=(t, mate), device_id_type=MESH)
    cnt_out = [pltpu.make_async_remote_copy(
        src_ref=cnt.at[0], dst_ref=cnt.at[d], send_sem=sc, recv_sem=rc,
        device_id=((t + d) % ntok, e), device_id_type=MESH) for d in range(1, ntok)]
    rest = pl.ds(1, ntok - 1)
    cnt_all = pltpu.make_async_remote_copy(
        src_ref=cnt.at[rest], dst_ref=cnt.at[rest], send_sem=sc, recv_sem=rc,
        device_id=(t, mate), device_id_type=MESH)
    fin_out = [pltpu.make_async_remote_copy(
        src_ref=fin.at[j], dst_ref=fin.at[3], send_sem=sc, recv_sem=rc,
        device_id=(t, k), device_id_type=MESH) for j, k in enumerate(others)]
    fin_all = pltpu.make_async_remote_copy(
        src_ref=fin.at[pl.ds(0, 3)], dst_ref=fin.at[pl.ds(0, 3)], send_sem=sc, recv_sem=rc,
        device_id=(t, mate), device_id_type=MESH)

    @pl.when(is_root)
    def _():
        bias_in.start()
        for d in range(1, ntok):
            pl.semaphore_signal(barrier, inc=1, device_id=((t + d) % ntok, e), device_id_type=MESH)
        ids_in.wait()
        lanes = 128
        numbers = lax.broadcasted_iota(jnp.int32, (experts, lanes), 0).astype(F32).astype(jnp.bfloat16)
        one, zero = jnp.bfloat16(1), jnp.bfloat16(0)
        exact = 256 // top
        blocks = rows // lanes
        total = jnp.zeros((1, experts), F32)
        for g0 in range(0, blocks, exact):
            acc = jnp.zeros((experts, lanes), jnp.bfloat16)
            for g in range(g0, min(g0 + exact, blocks)):
                found = ids[:, pl.ds(g * lanes, lanes)].astype(F32).astype(jnp.bfloat16)
                for j in range(top):
                    acc = acc + jnp.where(found[j:j + 1] == numbers, one, zero)
            total = total + jnp.sum(acc.astype(F32).T, axis=0, keepdims=True)
        cnt[0] = total.astype(jnp.int32)
        bias_in.wait()

    @pl.when(jnp.logical_not(is_root))
    def _():
        pl.semaphore_wait(barrier, 3)
        pl.semaphore_signal(ready, inc=1, device_id=(t, ROOT), device_id_type=MESH)
        bias_out.start()
        ids_in.wait()

    queue = list(range(first_x, n))

    def more_tokens(freed):
        while queue and slot[queue[0]] in freed:
            x_in[queue.pop(0)].start()

    def send_counts():
        pl.semaphore_wait(barrier, ntok - 1)
        for copy in cnt_out:
            copy.start()

    def send_counts_soon():
        pl.when(jnp.logical_and(is_root, 2 * t >= ntok))(send_counts)

    def send_counts_late():
        pl.when(jnp.logical_and(is_root, 2 * t < ntok))(send_counts)

    def finish_counts():
        @pl.when(is_root)
        def _():
            cnt_all.wait()
            bias_back.wait_recv()
            total = cnt[0]
            for d in range(1, ntok):
                total = total + cnt[d]
            load = total.astype(F32)
            target = F32(ntok * rows * top)
            gap = target - F32(experts) * load
            sign = jnp.where(gap > 0, F32(1), jnp.where(gap < 0, F32(-1), F32(0)))
            bias = jnp.concatenate([bias_all[k] for k in range(4)], axis=1)
            for j in range(4):
                fin[j, 0] = load
                fin[j, 1] = bias + 0.001 * sign
            for copy in fin_out:
                copy.start()

    def close_counts():
        @pl.when(is_root)
        def _():
            fin_all.wait_send()

        @pl.when(jnp.logical_not(is_root))
        def _():
            fin_out[0].wait_recv()
            bias_out.wait_send()

        load_ref[...] = fin[3, 0]
        newb_ref[...] = fin[3, 1]

    def first(at, i):
        return pltpu.make_async_remote_copy(
            src_ref=part.at[1 - c, :, at], dst_ref=rx1.at[:, at],
            send_sem=s1, recv_sem=r1.at[i], device_id=(t, mate), device_id_type=MESH)

    def second(at, i):
        return pltpu.make_async_remote_copy(
            src_ref=tx2.at[:, at], dst_ref=rx2.at[:, at],
            send_sem=s2, recv_sem=r2.at[i], device_id=(t, peer), device_id_type=MESH)

    side = 256
    tiles = depth // side
    shares = [[(q, k) for q in (0, 1) for k in range(tiles)
               if (k < (tiles + 1 - i % 2) // 2) == (q == 0)] for i in range(n)]
    line = [[(i, k) for i in range(n) for p, k in shares[i] if p == q] for q in (0, 1)]
    where = [0, 0]

    def push(q):
        if where[q] < len(line[q]):
            k = line[q][where[q]][1]
            pltpu.matmul_push_rhs(wv[pl.ds(k * side, side), :], staging_register=where[q] % 2, mxu_index=q)

    def issue(i):
        x_in[i].wait()
        more_tokens([slot[i]])
        left = [[k for p, k in shares[i] if p == q] for q in (0, 1)]
        for step in range(max(map(len, left))):
            for q in (0, 1):
                if step < len(left[q]):
                    k = left[q][step]
                    mark = where[q] % 2
                    where[q] += 1
                    push(q)
                    pltpu.matmul_acc_lhs(accs[acc_of[i]][q], xv[cols(i), pl.ds(k * side, side)], load_staged_rhs=mark)

    def stage_a(i):
        if i + 1 < n:
            issue(i + 1)
        r = (pltpu.matmul_pop(accs[acc_of[i]][0]) + pltpu.matmul_pop(accs[acc_of[i]][1])).T
        for k in range(4):
            part[k % 2, pl.ds(k // 2 * own, own), cols(i)] = r[k * own:(k + 1) * own]
        mine_ids = ids[:, cols(i)]
        low, high = mine_ids & 7, mine_ids >> 3
        picked = jnp.zeros(mine_ids.shape, F32)
        for k in range(experts // 8):
            row = jnp.take_along_axis(r[8 * k:8 * k + 8], low, axis=0, mode="promise_in_bounds")
            picked = jnp.where(high == k, row, picked)
        for k in range(2):
            part[k, pl.ds(2 * own, top), cols(i)] = picked
        if i == 0:
            @pl.when(is_root)
            def _():
                pl.semaphore_wait(ready, 3)
        first(cols(i), i).start()

    bound = 2 * depth * TOKEN_BOUND * GATE_BOUND
    grain = TOP_CODE / bound ** 0.25

    def encode(v):
        size = lax.rsqrt(lax.rsqrt(jnp.abs(v) + F32(1e-30))) * F32(grain) + F32(0.5)
        return jnp.where(v < 0, -size, size).astype(jnp.int32)

    def decode(whole):
        u = whole.astype(F32)
        return (u * u * F32(grain ** -4)) * (u * jnp.abs(u))

    def stage_b(i):
        first(cols(i), i).wait_recv()
        theirs = pl.ds(pl.multiple_of((1 - y) * own, own), own)
        ours = pl.ds(pl.multiple_of(y * own, own), own)
        tops = pl.ds(2 * own, top)
        code = encode(part[c, theirs, cols(i)] + rx1[theirs, cols(i)])
        chosen = encode(part[c, tops, cols(i)] + rx1[tops, cols(i)])
        tx2[0:own, cols(i)] = code.astype(LINK)
        tx2[own:, cols(i)] = chosen.astype(LINK)
        second(cols(i), i).start()
        keep[:, cols(i)] = part[c, ours, cols(i)] + rx1[ours, cols(i)]
        mine[:, cols(i)] = decode(chosen)

    def stage_c(i):
        second(cols(i), i).wait_recv()
        code = decode(rx2[0:own, cols(i)].astype(jnp.int32))
        tail = decode(rx2[own:, cols(i)].astype(jnp.int32))
        chosen = 1.0 / (1.0 + jnp.exp(-(mine[:, cols(i)] + tail)))
        wtsv[:, cols(i)] = 2.5 * chosen / jnp.sum(chosen, axis=0, keepdims=True)
        affv[:, cols(i)] = 1.0 / (1.0 + jnp.exp(-(keep[:, cols(i)] + code)))

    for j, copy in enumerate(w_in):
        copy.wait()
        more_tokens([j])
    for q in (0, 1):
        push(q)
    issue(0)
    for kind, i in plan(n, 3):
        if kind == "a":
            stage_a(i)
        else:
            stage_b(i)
        if (kind, i) == ("a", 1):
            send_counts_soon()
        if (kind, i) == ("a", n - 1):
            send_counts_late()
    for i in range(n):
        if i == n - 2:
            finish_counts()
        stage_c(i)
    close_counts()
    every = pl.ds(0, rows)
    first(every, 0).wait_send()
    second(every, 0).wait_send()


def place(aff, wts, load, newb, aff_hbm, wts_hbm, load_hbm, newb_hbm, sem):
    copies = [pltpu.make_async_copy(a, b, sem.at[k]) for k, (a, b) in enumerate(
        ((aff, aff_hbm), (wts, wts_hbm), (load, load_hbm), (newb, newb_hbm)))]
    for copy in copies:
        copy.start()
    for copy in copies:
        copy.wait()


def local(ntok, tokens, gate_weight, expert_ids, expert_bias):
    rows, depth = tokens.shape
    experts = gate_weight.shape[1]
    own = expert_bias.shape[0]
    top = expert_ids.shape[1]
    piece = 256
    widths = [piece // 2] * 2 + [piece] * (rows // piece - 1)
    n = len(widths)
    dma = pltpu.SemaphoreType.DMA
    vm = pltpu.VMEM
    any_ = pl.BlockSpec(memory_space=pl.ANY)
    vmem = pl.BlockSpec(memory_space=pltpu.VMEM)
    shapes = ((own, rows), (top, rows), (1, experts), (1, experts))
    results = pl.pallas_call(
        functools.partial(kernel, ntok, widths),
        out_shape=tuple(pltpu.VMEM(shape, F32) for shape in shapes),
        in_specs=[any_] * 4,
        out_specs=(vmem,) * 4,
        scratch_shapes=[
            vm((rows, depth), tokens.dtype), vm((depth, experts), gate_weight.dtype),
            vm((top, rows), jnp.int32),
            vm((4, 1, own), F32),
            vm((2, 2 * own + top, rows), F32), vm((2 * own + top, rows), F32),
            vm((own, rows), F32), vm((top, rows), F32),
            vm((own + top, rows), LINK), vm((own + top, rows), LINK),
            vm((ntok, 1, experts), jnp.int32), vm((4, 2, 1, experts), F32),
            dma((W_CHUNKS + 4,)), dma, dma((n,)), dma, dma((n,)), dma, dma, dma, pltpu.SemaphoreType.REGULAR,
        ],
        compiler_params=pltpu.CompilerParams(
            collective_id=0, has_side_effects=True, vmem_limit_bytes=60 * 1024 * 1024),
    )(tokens, gate_weight, expert_ids.T, expert_bias.reshape(1, own))
    aff, wts, load, newb = pl.pallas_call(
        place,
        out_shape=tuple(jax.ShapeDtypeStruct(shape, F32) for shape in shapes),
        in_specs=[vmem] * 4,
        out_specs=(pl.BlockSpec(memory_space=pltpu.HBM),) * 4,
        scratch_shapes=[dma((4,))],
    )(*(pltpu.with_memory_space_constraint(r, pltpu.VMEM) for r in results))
    return aff.T, wts.T, load.reshape(experts), newb.reshape(experts)


def solution(mesh):
    in_specs = (P("tok", "exp"), P("exp", None), P("tok", None), P("exp"))
    out_specs = (P("tok", "exp"), P("tok", None), P(), P())
    return jax.shard_map(functools.partial(local, mesh.shape["tok"]), mesh=mesh,
                         in_specs=in_specs, out_specs=out_specs, check_vma=False)
```

time: 17.4 us -> 15.3 us (0.88)
  Pallas kernels: 16.6 us -> 14.5 us
    pallas_call x1, Pallas kernels: 15.8 us -> 13.7 us  [local(): pl.pallas_call(functools.partial(kernel, ntok, widths), out_shape=tuple((...]
where the time goes in v2:
time: 15.3 us; the launch traced here: 15.2 us
  Pallas kernels  14.5 us (95%)
  between operations  0.64 us (4%)
    pallas_call x1, Pallas kernels, local(): pl.pallas_call(functools.partial(kernel, ntok, widths), out_shape=tuple((...  13.7 us
    pallas_call x1, Pallas kernels, local(): pl.pallas_call(place, out_shape=tuple((jax.ShapeDtypeStruct(shape, F32) f...  0.84 us

profile of v2, /device:TPU:0, one launch (start us, length us, event | category | flops | bytes accessed | tf_op | source)
XLA Modules:
  0.0 15.2 jit_solution(5721057444992064348)
XLA Ops:
  0.6 13.7 %shard_map.75 = (f32[64,2048]{1,0:T(8,128)S(1)}, f32[8,2048]{1,0:T(8,128)S(1)}, f32[1,256]{1,0:T(1,128)S(1)}, f32[1,256]{1,0:T(1,128)S(1)}) custom-call(bf16[2048,1792]{1,0:T(8,128)(2,1)} %x_hbm.1, bf16[1792,256]{1,0:T(8,128)(2,1)} %w_hbm.1, s32[8,2048]{1,0:T(8,128)} %bitcast.6, f32[1,64]{1,0:T(1,128)} %bitcast.7), custom_call_target="tpu_custom_call" | custom-call | tf_op jit(solution)/shard_map/pallas_call | solution.py:313
  14.3 0.8 %shard_map.76 = (f32[64,2048]{1,0:T(8,128)}, f32[8,2048]{1,0:T(8,128)}, f32[1,256]{1,0:T(1,128)}, f32[1,256]{1,0:T(1,128)}) custom-call(f32[64,2048]{1,0:T(8,128)S(1)} %get-tuple-element.12.aff, f32[8,2048]{1,0:T(8,128)S(1)} %get-tuple-element.13.wts, f32[1,256]{1,0:T(1,128)S(1)} %get-tuple-element.14.load, f32[1,256]{1,0:T(1,128)S(1)} %get-tuple-element.15.newb), custom_call_target="tpu_custom_call" | custom-call | tf_op jit(solution)/shard_map/pallas_call | solution.py:331

commit v3 on v2

--- a/solution.py
+++ b/solution.py
@@ -13,35 +13,41 @@
 TOP_CODE = 32760.0
 TOKEN_BOUND, GATE_BOUND = 6.0, 0.0625
 W_CHUNKS = 4
+LAG = (2, 5)
+HELD = 4
+AHEAD = 4
 ROOT = 1
 
 
-def plan(n, ahead):
-    order = [("a", i) for i in range(ahead)]
-    for i in range(n):
-        order += [("b", i)] + ([("a", i + ahead)] if i + ahead < n else [])
+def plan(n):
+    turn = list(range(1, n))
+    turn.insert(min(3, n - 1), 0)
+    order = []
+    for i in range(n + max(LAG)):
+        if i < n:
+            order.append(("a", i))
+        order += [(core, turn[i - LAG[core]]) for core in (0, 1) if 0 <= i - LAG[core] < n]
     return order
 
 
 def kernel(ntok, widths, x_hbm, w_hbm, ids_hbm, bias_hbm,
            affv, wtsv, load_ref, newb_ref,
-           xv, wv, ids, bias_all, part, rx1, keep, mine, tx2, rx2, cnt, fin,
-           l_sem, s1, r1, s2, r2, sc, rc, rb, ready):
-    sizes = sorted(set(widths))
-    acc_of = []
-    for i, width in enumerate(widths):
-        acc_of.append(2 * sizes.index(width) + sum(w == width for w in widths[:i]) % 2)
+           xv, wv, ids, bias_all, part, rx1, keep, mine, tx2, rx2, tx3, rx3, cnt, fin,
+           l_sem, s1, r1, s2, r2, s3, r3, sc, rc, rb, ready):
+    units = [widths[0] // 2] * 2 + widths[1:]
+    sizes = sorted(set(units))
+    acc_of = [2 * sizes.index(unit) + sum(u == unit for u in units[:j]) % 2 for j, unit in enumerate(units)]
     specs = [tuple(pltpu.ACC(q)((width, 256), F32) for q in (0, 1)) for width in sizes for _ in range(2)]
-    pl.run_scoped(functools.partial(body, ntok, widths, acc_of, (
+    pl.run_scoped(functools.partial(body, ntok, widths, units, acc_of, (
         x_hbm, w_hbm, ids_hbm, bias_hbm, affv, wtsv, load_ref, newb_ref,
-        xv, wv, ids, bias_all, part, rx1, keep, mine, tx2, rx2, cnt, fin,
-        l_sem, s1, r1, s2, r2, sc, rc, rb, ready)), *specs)
-
-
-def body(ntok, widths, acc_of, refs, *accs):
+        xv, wv, ids, bias_all, part, rx1, keep, mine, tx2, rx2, tx3, rx3, cnt, fin,
+        l_sem, s1, r1, s2, r2, s3, r3, sc, rc, rb, ready)), *specs)
+
+
+def body(ntok, widths, units, acc_of, refs, *accs):
     (x_hbm, w_hbm, ids_hbm, bias_hbm, affv, wtsv, load_ref, newb_ref,
-     xv, wv, ids, bias_all, part, rx1, keep, mine, tx2, rx2, cnt, fin,
-     l_sem, s1, r1, s2, r2, sc, rc, rb, ready) = refs
+     xv, wv, ids, bias_all, part, rx1, keep, mine, tx2, rx2, tx3, rx3, cnt, fin,
+     l_sem, s1, r1, s2, r2, s3, r3, sc, rc, rb, ready) = refs
     own = bias_all.shape[2]
     top, rows = ids.shape
     depth = xv.shape[1]
@@ -51,6 +57,7 @@
     y, c = e // 2, e % 2
     mate = 2 * y + 1 - c
     peer = 2 * (1 - y) + c
+    cross = 2 * (1 - y) + 1 - c
     experts = 4 * own
     is_root = e == ROOT
     others = [k for k in range(4) if k != ROOT]
@@ -58,16 +65,20 @@
     def cols(i):
         return pl.ds(starts[i], widths[i])
 
+    nu = len(units)
+
+    def unit(j):
+        return pl.ds(sum(units[:j]), units[j])
+
     chunk = -(-depth // W_CHUNKS // 256) * 256
     chunks = [pl.ds(k, min(chunk, depth - k)) for k in range(0, depth, chunk)]
-    nw = len(chunks)
-    w_in = [pltpu.make_async_copy(w_hbm.at[k], wv.at[k], l_sem.at[j]) for j, k in enumerate(chunks)]
-    first_x = 3
-    slot = [nw + i if i < first_x else (i - first_x) % (nw + first_x) for i in range(n)]
-    x_in = [pltpu.make_async_copy(x_hbm.at[cols(i)], xv.at[cols(i)], l_sem.at[slot[i]]) for i in range(n)]
-    ids_in = pltpu.make_async_copy(ids_hbm, ids, l_sem.at[nw + first_x])
+    w_in = [pltpu.make_async_copy(w_hbm.at[k], wv.at[k], l_sem.at[0]) for k in chunks]
+    w_all = pltpu.make_async_copy(w_hbm, wv, l_sem.at[0])
+    ids_in = pltpu.make_async_copy(ids_hbm, ids, l_sem.at[1])
+    slot = [2 + i if i < AHEAD else 0 if i == AHEAD else 2 + (i - AHEAD - 1) % AHEAD for i in range(nu)]
+    x_in = [pltpu.make_async_copy(x_hbm.at[unit(j)], xv.at[unit(j)], l_sem.at[slot[j]]) for j in range(nu)]
     ids_in.start()
-    for copy in w_in + x_in[:first_x]:
+    for copy in w_in + x_in[:AHEAD]:
         copy.start()
 
     barrier = pltpu.get_barrier_semaphore()
@@ -127,10 +138,10 @@
         bias_out.start()
         ids_in.wait()
 
-    queue = list(range(first_x, n))
+    queue = list(range(AHEAD, nu))
 
     def more_tokens(freed):
-        while queue and slot[queue[0]] in freed:
+        if queue and slot[queue[0]] == freed:
             x_in[queue.pop(0)].start()
 
     def send_counts():
@@ -186,11 +197,22 @@
             src_ref=tx2.at[:, at], dst_ref=rx2.at[:, at],
             send_sem=s2, recv_sem=r2.at[i], device_id=(t, peer), device_id_type=MESH)
 
+    def across(j):
+        at = pl.ds(rows + sum(units[:j]), units[j])
+        return pltpu.make_async_remote_copy(
+            src_ref=tx2.at[:, at], dst_ref=rx2.at[:, at],
+            send_sem=s2, recv_sem=r2.at[0], device_id=(t, cross), device_id_type=MESH)
+
+    chosen_out = pltpu.make_async_remote_copy(
+        src_ref=tx3, dst_ref=rx3, send_sem=s3, recv_sem=r3, device_id=(t, peer), device_id_type=MESH)
+    hand_on = pltpu.make_async_remote_copy(
+        src_ref=rx3, dst_ref=rx3, send_sem=s3, recv_sem=r3, device_id=(t, mate), device_id_type=MESH)
+
     side = 256
     tiles = depth // side
     shares = [[(q, k) for q in (0, 1) for k in range(tiles)
-               if (k < (tiles + 1 - i % 2) // 2) == (q == 0)] for i in range(n)]
-    line = [[(i, k) for i in range(n) for p, k in shares[i] if p == q] for q in (0, 1)]
+               if (k < (tiles + 1 - i % 2) // 2) == (q == 0)] for i in range(nu)]
+    line = [[(i, k) for i in range(nu) for p, k in shares[i] if p == q] for q in (0, 1)]
     where = [0, 0]
 
     def push(q):
@@ -200,7 +222,7 @@
 
     def issue(i):
         x_in[i].wait()
-        more_tokens([slot[i]])
+        more_tokens(slot[i])
         left = [[k for p, k in shares[i] if p == q] for q in (0, 1)]
         for step in range(max(map(len, left))):
             for q in (0, 1):
@@ -209,27 +231,49 @@
                     mark = where[q] % 2
                     where[q] += 1
                     push(q)
-                    pltpu.matmul_acc_lhs(accs[acc_of[i]][q], xv[cols(i), pl.ds(k * side, side)], load_staged_rhs=mark)
-
-    def stage_a(i):
-        if i + 1 < n:
-            issue(i + 1)
-        r = (pltpu.matmul_pop(accs[acc_of[i]][0]) + pltpu.matmul_pop(accs[acc_of[i]][1])).T
+                    pltpu.matmul_acc_lhs(accs[acc_of[i]][q], xv[unit(i), pl.ds(k * side, side)], load_staged_rhs=mark)
+
+    def product(j):
+        at = unit(j)
+        if j + 1 < nu:
+            issue(j + 1)
+        r = (pltpu.matmul_pop(accs[acc_of[j]][0]) + pltpu.matmul_pop(accs[acc_of[j]][1])).T
         for k in range(4):
-            part[k % 2, pl.ds(k // 2 * own, own), cols(i)] = r[k * own:(k + 1) * own]
-        mine_ids = ids[:, cols(i)]
+            part[k % 2, pl.ds(k // 2 * own, own), at] = r[k * own:(k + 1) * own]
+
+    def pick(at):
+        mine_ids = ids[:, at]
         low, high = mine_ids & 7, mine_ids >> 3
         picked = jnp.zeros(mine_ids.shape, F32)
         for k in range(experts // 8):
-            row = jnp.take_along_axis(r[8 * k:8 * k + 8], low, axis=0, mode="promise_in_bounds")
+            block, line = divmod(8 * k, own)
+            rows8 = part[block % 2, pl.ds(block // 2 * own + line, 8), at]
+            row = jnp.take_along_axis(rows8, low, axis=0, mode="promise_in_bounds")
             picked = jnp.where(high == k, row, picked)
         for k in range(2):
-            part[k, pl.ds(2 * own, top), cols(i)] = picked
+            part[k, pl.ds(2 * own, top), at] = picked
+
+    def to_mate(i):
+        pick(cols(i))
+        first(cols(i), i).start()
+
+    def stage_a(i):
         if i == 0:
-            @pl.when(is_root)
-            def _():
-                pl.semaphore_wait(ready, 3)
-        first(cols(i), i).start()
+            for j in (0, 1):
+                product(j)
+                if j == 0:
+                    @pl.when(is_root)
+                    def _():
+                        pl.semaphore_wait(ready, 3)
+                tx2[:, unit(j)] = encode(part[c, theirs, unit(j)]).astype(LINK)
+                tx2[:, pl.ds(rows + sum(units[:j]), units[j])] = encode(part[1 - c, theirs, unit(j)]).astype(LINK)
+                second(unit(j), 0).start()
+                across(j).start()
+        else:
+            product(i + 1)
+            to_mate(i)
+        if i == 1:
+            to_mate(0)
 
     bound = 2 * depth * TOKEN_BOUND * GATE_BOUND
     grain = TOP_CODE / bound ** 0.25
@@ -242,50 +286,66 @@
         u = whole.astype(F32)
         return (u * u * F32(grain ** -4)) * (u * jnp.abs(u))
 
-    def stage_b(i):
+    theirs = pl.ds(pl.multiple_of((1 - y) * own, own), own)
+    ours = pl.ds(pl.multiple_of(y * own, own), own)
+    picks = pl.ds(2 * own, top)
+
+    def stage_b(i, core):
         first(cols(i), i).wait_recv()
-        theirs = pl.ds(pl.multiple_of((1 - y) * own, own), own)
-        ours = pl.ds(pl.multiple_of(y * own, own), own)
-        tops = pl.ds(2 * own, top)
-        code = encode(part[c, theirs, cols(i)] + rx1[theirs, cols(i)])
-        chosen = encode(part[c, tops, cols(i)] + rx1[tops, cols(i)])
-        tx2[0:own, cols(i)] = code.astype(LINK)
-        tx2[own:, cols(i)] = chosen.astype(LINK)
-        second(cols(i), i).start()
+        if i > 0:
+            tx2[:, cols(i)] = encode(part[c, theirs, cols(i)] + rx1[theirs, cols(i)]).astype(LINK)
+            if core == 0 or i < n - HELD:
+                second(cols(i), i).start()
+        chosen = encode(part[c, picks, cols(i)] + rx1[picks, cols(i)])
+        if core == 1:
+            tx3[:, cols(i)] = chosen.astype(LINK)
+        if core == 1 and i == n - 1:
+            chosen_out.start()
+            for k in range(n - HELD, n):
+                second(cols(k), k).start()
         keep[:, cols(i)] = part[c, ours, cols(i)] + rx1[ours, cols(i)]
         mine[:, cols(i)] = decode(chosen)
 
+    def weigh():
+        chosen = 1.0 / (1.0 + jnp.exp(-(mine[...] + decode(rx3[...].astype(jnp.int32)))))
+        wtsv[...] = 2.5 * chosen / jnp.sum(chosen, axis=0, keepdims=True)
+
     def stage_c(i):
-        second(cols(i), i).wait_recv()
-        code = decode(rx2[0:own, cols(i)].astype(jnp.int32))
-        tail = decode(rx2[own:, cols(i)].astype(jnp.int32))
-        chosen = 1.0 / (1.0 + jnp.exp(-(mine[:, cols(i)] + tail)))
-        wtsv[:, cols(i)] = 2.5 * chosen / jnp.sum(chosen, axis=0, keepdims=True)
-        affv[:, cols(i)] = 1.0 / (1.0 + jnp.exp(-(keep[:, cols(i)] + code)))
-
-    for j, copy in enumerate(w_in):
-        copy.wait()
-        more_tokens([j])
+        second(pl.ds(0, 2 * widths[0]) if i == 0 else cols(i), i).wait_recv()
+        logits = keep[:, cols(i)] + decode(rx2[:, cols(i)].astype(jnp.int32))
+        if i == 0:
+            logits = logits + decode(rx2[:, pl.ds(rows, widths[0])].astype(jnp.int32))
+        affv[:, cols(i)] = 1.0 / (1.0 + jnp.exp(-logits))
+
+    w_all.wait()
+    more_tokens(0)
     for q in (0, 1):
         push(q)
     issue(0)
-    for kind, i in plan(n, 3):
+    for kind, i in plan(n):
         if kind == "a":
             stage_a(i)
         else:
-            stage_b(i)
+            pl.when(c == kind)(functools.partial(stage_b, i, kind))
         if (kind, i) == ("a", 1):
             send_counts_soon()
         if (kind, i) == ("a", n - 1):
             send_counts_late()
     for i in range(n):
-        if i == n - 2:
+        if i == n - HELD:
+            @pl.when(c == 1)
+            def _():
+                chosen_out.wait()
+                hand_on.start()
             finish_counts()
+        if i == n - 1:
+            pl.when(c == 0)(hand_on.wait_recv)
+            weigh()
         stage_c(i)
     close_counts()
-    every = pl.ds(0, rows)
-    first(every, 0).wait_send()
-    second(every, 0).wait_send()
+    first(pl.ds(0, rows), 0).wait_send()
+    second(pl.ds(0, rows + widths[0]), 0).wait_send()
+    pl.when(c == 1)(hand_on.wait_send)
 
 
 def place(aff, wts, load, newb, aff_hbm, wts_hbm, load_hbm, newb_hbm, sem):
@@ -303,7 +363,7 @@
     own = expert_bias.shape[0]
     top = expert_ids.shape[1]
     piece = 256
-    widths = [piece // 2] * 2 + [piece] * (rows // piece - 1)
+    widths = [piece] * (rows // piece)
     n = len(widths)
     dma = pltpu.SemaphoreType.DMA
     vm = pltpu.VMEM
@@ -321,9 +381,11 @@
             vm((4, 1, own), F32),
             vm((2, 2 * own + top, rows), F32), vm((2 * own + top, rows), F32),
             vm((own, rows), F32), vm((top, rows), F32),
-            vm((own + top, rows), LINK), vm((own + top, rows), LINK),
+            vm((own, rows + piece), LINK), vm((own, rows + piece), LINK),
+            vm((top, rows), LINK), vm((top, rows), LINK),
             vm((ntok, 1, experts), jnp.int32), vm((4, 2, 1, experts), F32),
-            dma((W_CHUNKS + 4,)), dma, dma((n,)), dma, dma((n,)), dma, dma, dma, pltpu.SemaphoreType.REGULAR,
+            dma((2 + AHEAD,)), dma, dma((n,)), dma, dma((n,)), dma, dma, dma, dma, dma,
+            pltpu.SemaphoreType.REGULAR,
         ],
         compiler_params=pltpu.CompilerParams(
             collective_id=0, has_side_effects=True, vmem_limit_bytes=60 * 1024 * 1024),

time: 15.3 us -> 14.1 us (0.922)
  the two profiles are of different devices: /device:TPU:0 before, /device:TPU:1 now
where the time goes in v3:
time: 14.1 us; the launch traced here: 13.9 us
  Pallas kernels  13.3 us (94%)
  between operations  0.64 us (5%)
    pallas_call x1, Pallas kernels, local(): pl.pallas_call(functools.partial(kernel, ntok, widths), out_shape=tuple((...  12.5 us
    pallas_call x1, Pallas kernels, local(): pl.pallas_call(place, out_shape=tuple((jax.ShapeDtypeStruct(shape, F32) f...  0.84 us

profile of v3, /device:TPU:1, one launch (start us, length us, event | category | flops | bytes accessed | tf_op | source)
XLA Modules:
  0.0 13.9 jit_solution(9646771456078102710)
XLA Ops:
  0.6 12.5 %shard_map.75 = (f32[64,2048]{1,0:T(8,128)S(1)}, f32[8,2048]{1,0:T(8,128)S(1)}, f32[1,256]{1,0:T(1,128)S(1)}, f32[1,256]{1,0:T(1,128)S(1)}) custom-call(bf16[2048,1792]{1,0:T(8,128)(2,1)} %x_hbm.1, bf16[1792,256]{1,0:T(8,128)(2,1)} %w_hbm.1, s32[8,2048]{1,0:T(8,128)} %bitcast.6, f32[1,64]{1,0:T(1,128)} %bitcast.7), custom_call_target="tpu_custom_call" | custom-call | tf_op jit(solution)/shard_map/pallas_call | solution.py:373
  13.1 0.8 %shard_map.76 = (f32[64,2048]{1,0:T(8,128)}, f32[8,2048]{1,0:T(8,128)}, f32[1,256]{1,0:T(1,128)}, f32[1,256]{1,0:T(1,128)}) custom-call(f32[64,2048]{1,0:T(8,128)S(1)} %get-tuple-element.12.aff, f32[8,2048]{1,0:T(8,128)S(1)} %get-tuple-element.13.wts, f32[1,256]{1,0:T(1,128)S(1)} %get-tuple-element.14.load, f32[1,256]{1,0:T(1,128)S(1)} %get-tuple-element.15.newb), custom_call_target="tpu_custom_call" | custom-call | tf_op jit(solution)/shard_map/pallas_call | solution.py:393

commit v4 on v3

--- a/solution.py
+++ b/solution.py
@@ -13,7 +13,8 @@
 TOP_CODE = 32760.0
 TOKEN_BOUND, GATE_BOUND = 6.0, 0.0625
 W_CHUNKS = 4
-LAG = (2, 5)
+RAW_AT = (0, 2)
+LAG = (3, 5)
 HELD = 4
 AHEAD = 4
 ROOT = 1
@@ -23,10 +24,10 @@
     turn = list(range(1, n))
     turn.insert(min(3, n - 1), 0)
     order = []
-    for i in range(n + max(LAG)):
-        if i < n:
-            order.append(("a", i))
-        order += [(core, turn[i - LAG[core]]) for core in (0, 1) if 0 <= i - LAG[core] < n]
+    for j in range(n + max(LAG)):
+        if j <= n:
+            order.append(("a", j))
+        order += [(core, turn[j - LAG[core]]) for core in (0, 1) if 0 <= j - LAG[core] < n]
     return order
 
 
@@ -34,9 +35,13 @@
            affv, wtsv, load_ref, newb_ref,
            xv, wv, ids, bias_all, part, rx1, keep, mine, tx2, rx2, tx3, rx3, cnt, fin,
            l_sem, s1, r1, s2, r2, s3, r3, sc, rc, rb, ready):
-    units = [widths[0] // 2] * 2 + widths[1:]
-    sizes = sorted(set(units))
-    acc_of = [2 * sizes.index(unit) + sum(u == unit for u in units[:j]) % 2 for j, unit in enumerate(units)]
+    half = widths[0] // 2
+    units = [(sum(widths[:i]), widths[i], i) for i in range(1, len(widths))]
+    for k, place in enumerate(RAW_AT):
+        units.insert(place, (k * half, half, 0))
+    sizes = sorted({width for _, width, _ in units})
+    acc_of = [2 * sizes.index(width) + sum(w == width for _, w, _ in units[:j]) % 2
+              for j, (_, width, _) in enumerate(units)]
     specs = [tuple(pltpu.ACC(q)((width, 256), F32) for q in (0, 1)) for width in sizes for _ in range(2)]
     pl.run_scoped(functools.partial(body, ntok, widths, units, acc_of, (
         x_hbm, w_hbm, ids_hbm, bias_hbm, affv, wtsv, load_ref, newb_ref,
@@ -68,7 +73,7 @@
     nu = len(units)
 
     def unit(j):
-        return pl.ds(sum(units[:j]), units[j])
+        return pl.ds(*units[j][:2])
 
     chunk = -(-depth // W_CHUNKS // 256) * 256
     chunks = [pl.ds(k, min(chunk, depth - k)) for k in range(0, depth, chunk)]
@@ -198,7 +203,7 @@
             send_sem=s2, recv_sem=r2.at[i], device_id=(t, peer), device_id_type=MESH)
 
     def across(j):
-        at = pl.ds(rows + sum(units[:j]), units[j])
+        at = pl.ds(rows + units[j][0], units[j][1])
         return pltpu.make_async_remote_copy(
             src_ref=tx2.at[:, at], dst_ref=rx2.at[:, at],
             send_sem=s2, recv_sem=r2.at[0], device_id=(t, cross), device_id_type=MESH)
@@ -257,22 +262,21 @@
         pick(cols(i))
         first(cols(i), i).start()
 
-    def stage_a(i):
+    def stage_a(j):
+        product(j)
+        if j == 0:
+            @pl.when(is_root)
+            def _():
+                pl.semaphore_wait(ready, 3)
+        start, width, i = units[j]
         if i == 0:
-            for j in (0, 1):
-                product(j)
-                if j == 0:
-                    @pl.when(is_root)
-                    def _():
-                        pl.semaphore_wait(ready, 3)
-                tx2[:, unit(j)] = encode(part[c, theirs, unit(j)]).astype(LINK)
-                tx2[:, pl.ds(rows + sum(units[:j]), units[j])] = encode(part[1 - c, theirs, unit(j)]).astype(LINK)
-                second(unit(j), 0).start()
-                across(j).start()
+            tx2[:, unit(j)] = encode(part[c, theirs, unit(j)]).astype(LINK)
+            tx2[:, pl.ds(rows + start, width)] = encode(part[1 - c, theirs, unit(j)]).astype(LINK)
+            second(unit(j), 0).start()
+            across(j).start()
         else:
-            product(i + 1)
             to_mate(i)
-        if i == 1:
+        if j == RAW_AT[-1] + 1:
             to_mate(0)
 
     bound = 2 * depth * TOKEN_BOUND * GATE_BOUND
@@ -329,7 +333,7 @@
             pl.when(c == kind)(functools.partial(stage_b, i, kind))
         if (kind, i) == ("a", 1):
             send_counts_soon()
-        if (kind, i) == ("a", n - 1):
+        if (kind, i) == ("a", n):
             send_counts_late()
     for i in range(n):
         if i == n - HELD:

time: 14.1 us -> 14 us (level)
  no operation moved by 1% of the time
where the time goes in v4:
time: 14 us; the launch traced here: 13.8 us
  Pallas kernels  13.2 us (94%)
  between operations  0.64 us (5%)
    pallas_call x1, Pallas kernels, local(): pl.pallas_call(functools.partial(kernel, ntok, widths), out_shape=tuple((...  12.3 us
    pallas_call x1, Pallas kernels, local(): pl.pallas_call(place, out_shape=tuple((jax.ShapeDtypeStruct(shape, F32) f...  0.84 us

profile of v4, /device:TPU:1, one launch (start us, length us, event | category | flops | bytes accessed | tf_op | source)
XLA Modules:
  0.0 13.8 jit_solution(11118920187565578713)
XLA Ops:
  0.6 12.3 %shard_map.75 = (f32[64,2048]{1,0:T(8,128)S(1)}, f32[8,2048]{1,0:T(8,128)S(1)}, f32[1,256]{1,0:T(1,128)S(1)}, f32[1,256]{1,0:T(1,128)S(1)}) custom-call(bf16[2048,1792]{1,0:T(8,128)(2,1)} %x_hbm.1, bf16[1792,256]{1,0:T(8,128)(2,1)} %w_hbm.1, s32[8,2048]{1,0:T(8,128)} %bitcast.6, f32[1,64]{1,0:T(1,128)} %bitcast.7), custom_call_target="tpu_custom_call" | custom-call | tf_op jit(solution)/shard_map/pallas_call | solution.py:377
  13.0 0.8 %shard_map.76 = (f32[64,2048]{1,0:T(8,128)}, f32[8,2048]{1,0:T(8,128)}, f32[1,256]{1,0:T(1,128)}, f32[1,256]{1,0:T(1,128)}) custom-call(f32[64,2048]{1,0:T(8,128)S(1)} %get-tuple-element.12.aff, f32[8,2048]{1,0:T(8,128)S(1)} %get-tuple-element.13.wts, f32[1,256]{1,0:T(1,128)S(1)} %get-tuple-element.14.load, f32[1,256]{1,0:T(1,128)S(1)} %get-tuple-element.15.newb), custom_call_target="tpu_custom_call" | custom-call | tf_op jit(solution)/shard_map/pallas_call | solution.py:397

commit v5 on v4

--- a/solution.py
+++ b/solution.py
@@ -1,4 +1,5 @@
 import functools
+import math
 
 import jax
 import jax.numpy as jnp
@@ -14,15 +15,31 @@
 TOKEN_BOUND, GATE_BOUND = 6.0, 0.0625
 W_CHUNKS = 4
 RAW_AT = (0, 2)
+MATE_RUNS = (1, 1, 2, 1, 1, 2)
+PEER_RUNS = (1, 3, 2, 1, 1)
 LAG = (3, 5)
 HELD = 4
 AHEAD = 4
 ROOT = 1
 
 
-def plan(n):
+def grouped(items, sizes):
+    runs, at = [], 0
+    for size in list(sizes) + [1] * len(items):
+        if at < len(items):
+            runs.append(items[at:at + size])
+            at += size
+    return runs
+
+
+def turns(n):
     turn = list(range(1, n))
     turn.insert(min(3, n - 1), 0)
+    return turn
+
+
+def plan(n):
+    turn = turns(n)
     order = []
     for j in range(n + max(LAG)):
         if j <= n:
@@ -32,7 +49,7 @@
 
 
 def kernel(ntok, widths, x_hbm, w_hbm, ids_hbm, bias_hbm,
-           affv, wtsv, load_ref, newb_ref,
+           wide, thin,
            xv, wv, ids, bias_all, part, rx1, keep, mine, tx2, rx2, tx3, rx3, cnt, fin,
            l_sem, s1, r1, s2, r2, s3, r3, sc, rc, rb, ready):
     half = widths[0] // 2
@@ -44,13 +61,13 @@
               for j, (_, width, _) in enumerate(units)]
     specs = [tuple(pltpu.ACC(q)((width, 256), F32) for q in (0, 1)) for width in sizes for _ in range(2)]
     pl.run_scoped(functools.partial(body, ntok, widths, units, acc_of, (
-        x_hbm, w_hbm, ids_hbm, bias_hbm, affv, wtsv, load_ref, newb_ref,
+        x_hbm, w_hbm, ids_hbm, bias_hbm, wide, thin,
         xv, wv, ids, bias_all, part, rx1, keep, mine, tx2, rx2, tx3, rx3, cnt, fin,
         l_sem, s1, r1, s2, r2, s3, r3, sc, rc, rb, ready)), *specs)
 
 
 def body(ntok, widths, units, acc_of, refs, *accs):
-    (x_hbm, w_hbm, ids_hbm, bias_hbm, affv, wtsv, load_ref, newb_ref,
+    (x_hbm, w_hbm, ids_hbm, bias_hbm, wide, thin,
      xv, wv, ids, bias_all, part, rx1, keep, mine, tx2, rx2, tx3, rx3, cnt, fin,
      l_sem, s1, r1, s2, r2, s3, r3, sc, rc, rb, ready) = refs
     own = bias_all.shape[2]
@@ -71,9 +88,16 @@
         return pl.ds(starts[i], widths[i])
 
     nu = len(units)
+    mate_runs, peer_runs = grouped(turns(n), MATE_RUNS), grouped(list(range(n)), PEER_RUNS)
+    mate_run = {i: k for k, run in enumerate(mate_runs) for i in run}
+    peer_run = {i: k for k, run in enumerate(peer_runs) for i in run}
 
     def unit(j):
         return pl.ds(*units[j][:2])
+
+    def within(j):
+        start, width, i = units[j]
+        return pl.ds(start - starts[i], width)
 
     chunk = -(-depth // W_CHUNKS // 256) * 256
     chunks = [pl.ds(k, min(chunk, depth - k)) for k in range(0, depth, chunk)]
@@ -189,29 +213,37 @@
             fin_out[0].wait_recv()
             bias_out.wait_send()
 
-        load_ref[...] = fin[3, 0]
-        newb_ref[...] = fin[3, 1]
-
-    def first(at, i):
+        thin[...] = fin[3]
+
+    def first(at, k):
         return pltpu.make_async_remote_copy(
-            src_ref=part.at[1 - c, :, at], dst_ref=rx1.at[:, at],
-            send_sem=s1, recv_sem=r1.at[i], device_id=(t, mate), device_id_type=MESH)
-
-    def second(at, i):
+            src_ref=part.at[1 - c, at], dst_ref=rx1.at[at],
+            send_sem=s1, recv_sem=r1.at[k], device_id=(t, mate), device_id_type=MESH)
+
+    def second(at, k):
         return pltpu.make_async_remote_copy(
-            src_ref=tx2.at[:, at], dst_ref=rx2.at[:, at],
-            send_sem=s2, recv_sem=r2.at[i], device_id=(t, peer), device_id_type=MESH)
+            src_ref=tx2.at[at], dst_ref=rx2.at[at],
+            send_sem=s2, recv_sem=r2.at[k], device_id=(t, peer), device_id_type=MESH)
+
+    def raw(j):
+        return pltpu.make_async_remote_copy(
+            src_ref=tx2.at[0, :, within(j)], dst_ref=rx2.at[0, :, within(j)],
+            send_sem=s2, recv_sem=r2.at[0], device_id=(t, peer), device_id_type=MESH)
 
     def across(j):
-        at = pl.ds(rows + units[j][0], units[j][1])
         return pltpu.make_async_remote_copy(
-            src_ref=tx2.at[:, at], dst_ref=rx2.at[:, at],
+            src_ref=tx2.at[n, :, within(j)], dst_ref=rx2.at[n, :, within(j)],
             send_sem=s2, recv_sem=r2.at[0], device_id=(t, cross), device_id_type=MESH)
 
     chosen_out = pltpu.make_async_remote_copy(
         src_ref=tx3, dst_ref=rx3, send_sem=s3, recv_sem=r3, device_id=(t, peer), device_id_type=MESH)
     hand_on = pltpu.make_async_remote_copy(
         src_ref=rx3, dst_ref=rx3, send_sem=s3, recv_sem=r3, device_id=(t, mate), device_id_type=MESH)
+
+    def arrival(i, runs, copy, blocks):
+        for k, run in enumerate(runs):
+            if run[0] == i:
+                copy(pl.ds(0, sum(blocks(m) for m in run)), k).wait_recv()
 
     side = 256
     tiles = depth // side
@@ -239,28 +271,27 @@
                     pltpu.matmul_acc_lhs(accs[acc_of[i]][q], xv[unit(i), pl.ds(k * side, side)], load_staged_rhs=mark)
 
     def product(j):
-        at = unit(j)
-        if j + 1 < nu:
+        if 0 < j < nu - 1:
             issue(j + 1)
         r = (pltpu.matmul_pop(accs[acc_of[j]][0]) + pltpu.matmul_pop(accs[acc_of[j]][1])).T
         for k in range(4):
-            part[k % 2, pl.ds(k // 2 * own, own), at] = r[k * own:(k + 1) * own]
-
-    def pick(at):
-        mine_ids = ids[:, at]
+            part[k % 2, units[j][2], pl.ds(k // 2 * own, own), within(j)] = r[k * own:(k + 1) * own]
+
+    def pick(i):
+        mine_ids = ids[:, cols(i)]
         low, high = mine_ids & 7, mine_ids >> 3
         picked = jnp.zeros(mine_ids.shape, F32)
         for k in range(experts // 8):
             block, line = divmod(8 * k, own)
-            rows8 = part[block % 2, pl.ds(block // 2 * own + line, 8), at]
+            rows8 = part[block % 2, i, pl.ds(block // 2 * own + line, 8), :]
             row = jnp.take_along_axis(rows8, low, axis=0, mode="promise_in_bounds")
             picked = jnp.where(high == k, row, picked)
         for k in range(2):
-            part[k, pl.ds(2 * own, top), at] = picked
+            part[k, i, pl.ds(2 * own, top), :] = picked
 
     def to_mate(i):
-        pick(cols(i))
-        first(cols(i), i).start()
+        pick(i)
+        first(i, mate_run[i]).start()
 
     def stage_a(j):
         product(j)
@@ -270,56 +301,59 @@
                 pl.semaphore_wait(ready, 3)
         start, width, i = units[j]
         if i == 0:
-            tx2[:, unit(j)] = encode(part[c, theirs, unit(j)]).astype(LINK)
-            tx2[:, pl.ds(rows + start, width)] = encode(part[1 - c, theirs, unit(j)]).astype(LINK)
-            second(unit(j), 0).start()
+            tx2[0, :, within(j)] = encode(part[c, 0, theirs, within(j)]).astype(LINK)
+            tx2[n, :, within(j)] = encode(part[1 - c, 0, theirs, within(j)]).astype(LINK)
+            raw(j).start()
             across(j).start()
         else:
             to_mate(i)
+        if j == 0:
+            issue(1)
         if j == RAW_AT[-1] + 1:
             to_mate(0)
 
     bound = 2 * depth * TOKEN_BOUND * GATE_BOUND
-    grain = TOP_CODE / bound ** 0.25
+    grain = TOP_CODE / math.asinh(bound)
 
     def encode(v):
-        size = lax.rsqrt(lax.rsqrt(jnp.abs(v) + F32(1e-30))) * F32(grain) + F32(0.5)
-        return jnp.where(v < 0, -size, size).astype(jnp.int32)
+        size = jnp.abs(v)
+        code = jnp.log(size + jnp.sqrt(size * size + F32(1))) * F32(grain) + F32(0.5)
+        return jnp.where(v < 0, -code, code).astype(jnp.int32)
 
     def decode(whole):
-        u = whole.astype(F32)
-        return (u * u * F32(grain ** -4)) * (u * jnp.abs(u))
+        grown = jnp.exp(whole.astype(F32) * F32(1 / grain))
+        return F32(0.5) * grown - F32(0.5) / grown
 
     theirs = pl.ds(pl.multiple_of((1 - y) * own, own), own)
     ours = pl.ds(pl.multiple_of(y * own, own), own)
     picks = pl.ds(2 * own, top)
 
     def stage_b(i, core):
-        first(cols(i), i).wait_recv()
+        arrival(i, mate_runs, first, lambda m: 1)
         if i > 0:
-            tx2[:, cols(i)] = encode(part[c, theirs, cols(i)] + rx1[theirs, cols(i)]).astype(LINK)
+            tx2[i] = encode(part[c, i, theirs] + rx1[i, theirs]).astype(LINK)
             if core == 0 or i < n - HELD:
-                second(cols(i), i).start()
-        chosen = encode(part[c, picks, cols(i)] + rx1[picks, cols(i)])
+                second(i, peer_run[i]).start()
+        chosen = encode(part[c, i, picks] + rx1[i, picks])
         if core == 1:
             tx3[:, cols(i)] = chosen.astype(LINK)
         if core == 1 and i == n - 1:
             chosen_out.start()
             for k in range(n - HELD, n):
-                second(cols(k), k).start()
-        keep[:, cols(i)] = part[c, ours, cols(i)] + rx1[ours, cols(i)]
+                second(k, peer_run[k]).start()
+        keep[:, cols(i)] = part[c, i, ours] + rx1[i, ours]
         mine[:, cols(i)] = decode(chosen)
 
     def weigh():
         chosen = 1.0 / (1.0 + jnp.exp(-(mine[...] + decode(rx3[...].astype(jnp.int32)))))
-        wtsv[...] = 2.5 * chosen / jnp.sum(chosen, axis=0, keepdims=True)
+        wide[own:] = 2.5 * chosen / jnp.sum(chosen, axis=0, keepdims=True)
 
     def stage_c(i):
-        second(pl.ds(0, 2 * widths[0]) if i == 0 else cols(i), i).wait_recv()
-        logits = keep[:, cols(i)] + decode(rx2[:, cols(i)].astype(jnp.int32))
+        arrival(i, peer_runs, second, lambda m: 2 if m == 0 else 1)
+        logits = keep[:, cols(i)] + decode(rx2[i].astype(jnp.int32))
         if i == 0:
-            logits = logits + decode(rx2[:, pl.ds(rows, widths[0])].astype(jnp.int32))
-        affv[:, cols(i)] = 1.0 / (1.0 + jnp.exp(-logits))
+            logits = logits + decode(rx2[n].astype(jnp.int32))
+        wide[0:own, cols(i)] = 1.0 / (1.0 + jnp.exp(-logits))
 
     w_all.wait()
     more_tokens(0)
@@ -347,18 +381,19 @@
             weigh()
         stage_c(i)
     close_counts()
-    first(pl.ds(0, rows), 0).wait_send()
-    second(pl.ds(0, rows + widths[0]), 0).wait_send()
+    first(pl.ds(0, n), 0).wait_send()
+    second(pl.ds(0, n + 1), 0).wait_send()
     pl.when(c == 1)(hand_on.wait_send)
 
 
-def place(aff, wts, load, newb, aff_hbm, wts_hbm, load_hbm, newb_hbm, sem):
-    copies = [pltpu.make_async_copy(a, b, sem.at[k]) for k, (a, b) in enumerate(
-        ((aff, aff_hbm), (wts, wts_hbm), (load, load_hbm), (newb, newb_hbm)))]
-    for copy in copies:
-        copy.start()
-    for copy in copies:
-        copy.wait()
+def place(wide, thin, aff_hbm, wts_hbm, load_hbm, newb_hbm, sem):
+    for k, (source, results) in enumerate(((wide, (aff_hbm, wts_hbm)), (thin, (load_hbm, newb_hbm)))):
+        at = 0
+        for result in results:
+            pltpu.make_async_copy(source.at[pl.ds(at, result.shape[0])], result, sem.at[k]).start()
+            at += result.shape[0]
+    for k, source in enumerate((wide, thin)):
+        pltpu.make_async_copy(source, source, sem.at[k]).wait()
 
 
 def local(ntok, tokens, gate_weight, expert_ids, expert_bias):
@@ -373,22 +408,23 @@
     vm = pltpu.VMEM
     any_ = pl.BlockSpec(memory_space=pl.ANY)
     vmem = pl.BlockSpec(memory_space=pltpu.VMEM)
-    shapes = ((own, rows), (top, rows), (1, experts), (1, experts))
+    shapes = ((own, rows), (top, rows), (1, 1, experts), (1, 1, experts))
     results = pl.pallas_call(
         functools.partial(kernel, ntok, widths),
-        out_shape=tuple(pltpu.VMEM(shape, F32) for shape in shapes),
+        out_shape=(pltpu.VMEM((own + top, rows), F32), pltpu.VMEM((2, 1, experts), F32)),
         in_specs=[any_] * 4,
-        out_specs=(vmem,) * 4,
+        out_specs=(vmem,) * 2,
         scratch_shapes=[
             vm((rows, depth), tokens.dtype), vm((depth, experts), gate_weight.dtype),
             vm((top, rows), jnp.int32),
             vm((4, 1, own), F32),
-            vm((2, 2 * own + top, rows), F32), vm((2 * own + top, rows), F32),
+            vm((2, n, 2 * own + top, piece), F32), vm((n, 2 * own + top, piece), F32),
             vm((own, rows), F32), vm((top, rows), F32),
-            vm((own, rows + piece), LINK), vm((own, rows + piece), LINK),
+            vm((n + 1, own, piece), LINK), vm((n + 1, own, piece), LINK),
             vm((top, rows), LINK), vm((top, rows), LINK),
             vm((ntok, 1, experts), jnp.int32), vm((4, 2, 1, experts), F32),
-            dma((2 + AHEAD,)), dma, dma((n,)), dma, dma((n,)), dma, dma, dma, dma, dma,
+            dma((2 + AHEAD,)), dma, dma((len(grouped(turns(n), MATE_RUNS)),)),
+            dma, dma((len(grouped(turns(n), PEER_RUNS)),)), dma, dma, dma, dma, dma,
             pltpu.SemaphoreType.REGULAR,
         ],
         compiler_params=pltpu.CompilerParams(
@@ -397,9 +433,9 @@
     aff, wts, load, newb = pl.pallas_call(
         place,
         out_shape=tuple(jax.ShapeDtypeStruct(shape, F32) for shape in shapes),
-        in_specs=[vmem] * 4,
+        in_specs=[vmem] * 2,
         out_specs=(pl.BlockSpec(memory_space=pltpu.HBM),) * 4,
-        scratch_shapes=[dma((4,))],
+        scratch_shapes=[dma((2,))],
     )(*(pltpu.with_memory_space_constraint(r, pltpu.VMEM) for r in results))
     return aff.T, wts.T, load.reshape(experts), newb.reshape(experts)
 

time: 14 us -> 14 us (level)
  no operation moved by 1% of the time
where the time goes in v5:
time: 14 us; the launch traced here: 13.8 us
  Pallas kernels  13.2 us (94%)
  between operations  0.64 us (5%)
    pallas_call x1, Pallas kernels, local(): pl.pallas_call(functools.partial(kernel, ntok, widths), out_shape=(pltpu....  12.4 us
    pallas_call x1, Pallas kernels, local(): pl.pallas_call(place, out_shape=tuple((jax.ShapeDtypeStruct(shape, F32) f...  0.82 us

profile of v5, /device:TPU:1, one launch (start us, length us, event | category | flops | bytes accessed | tf_op | source)
XLA Modules:
  0.0 13.8 jit_solution(7511609267704396332)
XLA Ops:
  0.6 12.4 %shard_map.75 = (f32[72,2048]{1,0:T(8,128)S(1)}, f32[2,1,256]{2,1,0:T(1,128)S(1)}) custom-call(bf16[2048,1792]{1,0:T(8,128)(2,1)} %x_hbm.1, bf16[1792,256]{1,0:T(8,128)(2,1)} %w_hbm.1, s32[8,2048]{1,0:T(8,128)} %bitcast.6, f32[1,64]{1,0:T(1,128)} %bitcast.7), custom_call_target="tpu_custom_call" | custom-call | tf_op jit(solution)/shard_map/pallas_call | solution.py:412
  13.0 0.8 %shard_map.76 = (f32[64,2048]{1,0:T(8,128)}, f32[8,2048]{1,0:T(8,128)}, f32[1,1,256]{2,1,0:T(1,128)}, f32[1,1,256]{2,1,0:T(1,128)}) custom-call(f32[72,2048]{1,0:T(8,128)S(1)} %get-tuple-element.10.wide, f32[2,1,256]{2,1,0:T(1,128)S(1)} %get-tuple-element.11.thin), custom_call_target="tpu_custom_call" | custom-call | tf_op jit(solution)/shard_map/pallas_call | solution.py:433

commit v6 on v5

--- a/solution.py
+++ b/solution.py
@@ -15,7 +15,7 @@
 TOKEN_BOUND, GATE_BOUND = 6.0, 0.0625
 W_CHUNKS = 4
 RAW_AT = (0, 2)
-MATE_RUNS = (1, 1, 2, 1, 1, 2)
+MATE_RUNS = (1, 1, 1, 2, 1, 2)
 PEER_RUNS = (1, 3, 2, 1, 1)
 LAG = (3, 5)
 HELD = 4
@@ -34,7 +34,7 @@
 
 def turns(n):
     turn = list(range(1, n))
-    turn.insert(min(3, n - 1), 0)
+    turn.insert(min(4, n - 1), 0)
     return turn
 
 

time: 14 us -> 14 us (level)
  no operation moved by 1% of the time
where the time goes in v6:
time: 14 us; the launch traced here: 13.8 us
  Pallas kernels  13.2 us (94%)
  between operations  0.64 us (5%)
    pallas_call x1, Pallas kernels, local(): pl.pallas_call(functools.partial(kernel, ntok, widths), out_shape=(pltpu....  12.4 us
    pallas_call x1, Pallas kernels, local(): pl.pallas_call(place, out_shape=tuple((jax.ShapeDtypeStruct(shape, F32) f...  0.82 us

profile of v6, /device:TPU:1, one launch (start us, length us, event | category | flops | bytes accessed | tf_op | source)
XLA Modules:
  0.0 13.8 jit_solution(2674532811011615999)
XLA Ops:
  0.6 12.4 %shard_map.75 = (f32[72,2048]{1,0:T(8,128)S(1)}, f32[2,1,256]{2,1,0:T(1,128)S(1)}) custom-call(bf16[2048,1792]{1,0:T(8,128)(2,1)} %x_hbm.1, bf16[1792,256]{1,0:T(8,128)(2,1)} %w_hbm.1, s32[8,2048]{1,0:T(8,128)} %bitcast.6, f32[1,64]{1,0:T(1,128)} %bitcast.7), custom_call_target="tpu_custom_call" | custom-call | tf_op jit(solution)/shard_map/pallas_call | solution.py:412
  13.0 0.8 %shard_map.76 = (f32[64,2048]{1,0:T(8,128)}, f32[8,2048]{1,0:T(8,128)}, f32[1,1,256]{2,1,0:T(1,128)}, f32[1,1,256]{2,1,0:T(1,128)}) custom-call(f32[72,2048]{1,0:T(8,128)S(1)} %get-tuple-element.10.wide, f32[2,1,256]{2,1,0:T(1,128)S(1)} %get-tuple-element.11.thin), custom_call_target="tpu_custom_call" | custom-call | tf_op jit(solution)/shard_map/pallas_call | solution.py:433

commit v7 on v6

--- a/solution.py
+++ b/solution.py
@@ -379,11 +379,11 @@
         if i == n - 1:
             pl.when(c == 0)(hand_on.wait_recv)
             weigh()
+            close_counts()
+            first(pl.ds(0, n), 0).wait_send()
+            second(pl.ds(0, n + 1), 0).wait_send()
+            pl.when(c == 1)(hand_on.wait_send)
         stage_c(i)
-    close_counts()
-    first(pl.ds(0, n), 0).wait_send()
-    second(pl.ds(0, n + 1), 0).wait_send()
-    pl.when(c == 1)(hand_on.wait_send)
 
 
 def place(wide, thin, aff_hbm, wts_hbm, load_hbm, newb_hbm, sem):

time: 14 us -> 14 us (level)
  no operation moved by 1% of the time
where the time goes in v7:
time: 14 us; the launch traced here: 13.8 us
  Pallas kernels  13.2 us (94%)
  between operations  0.64 us (5%)
    pallas_call x1, Pallas kernels, local(): pl.pallas_call(functools.partial(kernel, ntok, widths), out_shape=(pltpu....  12.4 us
    pallas_call x1, Pallas kernels, local(): pl.pallas_call(place, out_shape=tuple((jax.ShapeDtypeStruct(shape, F32) f...  0.82 us

profile of v7, /device:TPU:1, one launch (start us, length us, event | category | flops | bytes accessed | tf_op | source)
XLA Modules:
  0.0 13.8 jit_solution(7898023846860493428)
XLA Ops:
  0.6 12.4 %shard_map.75 = (f32[72,2048]{1,0:T(8,128)S(1)}, f32[2,1,256]{2,1,0:T(1,128)S(1)}) custom-call(bf16[2048,1792]{1,0:T(8,128)(2,1)} %x_hbm.1, bf16[1792,256]{1,0:T(8,128)(2,1)} %w_hbm.1, s32[8,2048]{1,0:T(8,128)} %bitcast.6, f32[1,64]{1,0:T(1,128)} %bitcast.7), custom_call_target="tpu_custom_call" | custom-call | tf_op jit(solution)/shard_map/pallas_call | solution.py:412
  13.0 0.8 %shard_map.76 = (f32[64,2048]{1,0:T(8,128)}, f32[8,2048]{1,0:T(8,128)}, f32[1,1,256]{2,1,0:T(1,128)}, f32[1,1,256]{2,1,0:T(1,128)}) custom-call(f32[72,2048]{1,0:T(8,128)S(1)} %get-tuple-element.10.wide, f32[2,1,256]{2,1,0:T(1,128)S(1)} %get-tuple-element.11.thin), custom_call_target="tpu_custom_call" | custom-call | tf_op jit(solution)/shard_map/pallas_call | solution.py:433

commit v8 on v7

--- a/solution.py
+++ b/solution.py
@@ -13,13 +13,13 @@
 LINK = jnp.int16
 TOP_CODE = 32760.0
 TOKEN_BOUND, GATE_BOUND = 6.0, 0.0625
-W_CHUNKS = 4
+W_CHUNKS = 2
 RAW_AT = (0, 2)
 MATE_RUNS = (1, 1, 1, 2, 1, 2)
 PEER_RUNS = (1, 3, 2, 1, 1)
 LAG = (3, 5)
 HELD = 4
-AHEAD = 4
+AHEAD = 5
 ROOT = 1
 
 

time: 14 us -> 14 us (level)
  no operation moved by 1% of the time
where the time goes in v8:
time: 14 us; the launch traced here: 13.9 us
  Pallas kernels  13.2 us (94%)
  between operations  0.64 us (5%)
    pallas_call x1, Pallas kernels, local(): pl.pallas_call(functools.partial(kernel, ntok, widths), out_shape=(pltpu....  12.4 us
    pallas_call x1, Pallas kernels, local(): pl.pallas_call(place, out_shape=tuple((jax.ShapeDtypeStruct(shape, F32) f...  0.82 us

profile of v8, /device:TPU:1, one launch (start us, length us, event | category | flops | bytes accessed | tf_op | source)
XLA Modules:
  0.0 13.9 jit_solution(17946742093085082189)
XLA Ops:
  0.6 12.4 %shard_map.75 = (f32[72,2048]{1,0:T(8,128)S(1)}, f32[2,1,256]{2,1,0:T(1,128)S(1)}) custom-call(bf16[2048,1792]{1,0:T(8,128)(2,1)} %x_hbm.1, bf16[1792,256]{1,0:T(8,128)(2,1)} %w_hbm.1, s32[8,2048]{1,0:T(8,128)} %bitcast.6, f32[1,64]{1,0:T(1,128)} %bitcast.7), custom_call_target="tpu_custom_call" | custom-call | tf_op jit(solution)/shard_map/pallas_call | solution.py:412
  13.0 0.8 %shard_map.76 = (f32[64,2048]{1,0:T(8,128)}, f32[8,2048]{1,0:T(8,128)}, f32[1,1,256]{2,1,0:T(1,128)}, f32[1,1,256]{2,1,0:T(1,128)}) custom-call(f32[72,2048]{1,0:T(8,128)S(1)} %get-tuple-element.10.wide, f32[2,1,256]{2,1,0:T(1,128)S(1)} %get-tuple-element.11.thin), custom_call_target="tpu_custom_call" | custom-call | tf_op jit(solution)/shard_map/pallas_call | solution.py:433
